TPU v7x, 32 devices: a whole 2x2x4 slice. The times are simulated.
32 devices in a mesh: gx: 4 (over y, core), gy: 4 (over z), gz: 2 (over x).
Axes of the slice: x: 2, y: 2, z: 4, core: 2. Of those that a mesh axis runs over, the one named last changes fastest.
Arguments:
- stream: bfloat16 [8192, 8192], P(('gx', 'gy', 'gz')), may hold values from -4 to 4
- segment_ids: int32 [8192], P(('gx', 'gy', 'gz')), may hold values from 0 to 8191, as said below
- positions: int32 [8192], P(('gx', 'gy', 'gz')), may hold values from 0 to 255, as said below
- norm_gain: bfloat16 [1, 8192], P(None, ('gx', 'gy', 'gz')), may hold values from 0.099609375 to 1.8984375
- q_weight: bfloat16 [1, 8192, 512], P(None, ('gx', 'gy', 'gz')), as said below
- k_weight: bfloat16 [1, 8192, 128], P(None, ('gx', 'gy', 'gz')), as said below
- v_weight: bfloat16 [1, 8192, 128], P(None, ('gx', 'gy', 'gz')), may hold values from -0.0625 to 0.0625
- o_weight: bfloat16 [1, 512, 8192], P(None, None, ('gx', 'gy', 'gz')), may hold values from -0.25 to 0.25
Outputs:
- result: bfloat16 [8192, 8192], P(('gx', 'gy', 'gz'))
Inputs may be any that keep to these rules, and one draw needn't show every extreme that they name: `segment_ids`: each token's id is the index of its document's first token, so ids never fall along the tokens; every document lies inside one aligned block of 256 tokens, every block starts a new document, and the last token is a document of its own. `positions`: counts from 0 at a document's first token and rises by one per token. `q_weight`: A projection scaled by its fan-in. `k_weight`: A projection scaled by its fan-in.
All inputs are finite; a program needn't handle non-finite values.
Results may differ from a plain program's by a relative error of at most 0.0064.
Values may be sent and summed in bfloat16 or wider, within the bound.
A program may use at most 128 MiB of HBM per device.

v0:
```python
import math
import jax
import jax.numpy as jnp
from jax import lax
from jax.sharding import PartitionSpec as P


def rotate(values, positions):
    width = values.shape[-1]
    half = width // 2
    freqs = jnp.exp(-math.log(500000.0) * jnp.arange(half, dtype=jnp.float32) * 2.0 / width)
    angles = positions.astype(jnp.float32)[:, None] * freqs[None, :]
    cosine = jnp.concatenate([jnp.cos(angles), jnp.cos(angles)], -1)[:, None, :]
    sine = jnp.concatenate([jnp.sin(angles), jnp.sin(angles)], -1)[:, None, :]
    turned = jnp.concatenate([-values[..., half:], values[..., :half]], -1)
    return values * cosine + turned * sine


def attend(queries, keys, values, segment_ids, positions):
    count = queries.shape[0]
    scores = jnp.einsum(
        "thd,sd->hts", queries, keys, preferred_element_type=jnp.float32
    ) / math.sqrt(keys.shape[-1])
    allowed = (segment_ids[:, None] == segment_ids[None, :]) & (
        positions[None, :] <= positions[:, None]
    )
    scores = jnp.where(allowed[None], scores, -1e30)
    peak = jnp.max(scores, -1, keepdims=True)
    expd = jnp.exp(scores - peak)
    probs = (expd / jnp.sum(expd, -1, keepdims=True)).astype(jnp.bfloat16)
    mixed = jnp.einsum("hts,sd->thd", probs, values, preferred_element_type=jnp.float32)
    return mixed.astype(jnp.bfloat16).reshape(count, -1)


def body(stream, segment_ids, positions, norm_gain, q_weight, k_weight, v_weight, o_weight):
    count = stream.shape[0]
    head_size = k_weight.shape[2]
    current = stream
    widened = lax.optimization_barrier(current).astype(jnp.float32)
    inverse = lax.rsqrt(jnp.mean(widened * widened, -1, keepdims=True) + 1e-05)
    scaled = widened * inverse
    inner = (
        lax.all_gather(norm_gain[0], "gz", axis=0, tiled=True),
        lax.all_gather(q_weight[0], "gz", axis=0, tiled=True),
        lax.all_gather(k_weight[0], "gz", axis=0, tiled=True),
        lax.all_gather(v_weight[0], "gz", axis=0, tiled=True),
    )
    middle = (
        lax.all_gather(inner[0], "gy", axis=0, tiled=True),
        lax.all_gather(inner[1], "gy", axis=0, tiled=True),
        lax.all_gather(inner[2], "gy", axis=0, tiled=True),
        lax.all_gather(inner[3], "gy", axis=0, tiled=True),
    )
    gain_piece = lax.all_gather(middle[0], "gx", axis=0, tiled=True)
    query_piece = lax.all_gather(middle[1], "gx", axis=0, tiled=True)
    key_piece = lax.all_gather(middle[2], "gx", axis=0, tiled=True)
    value_piece = lax.all_gather(middle[3], "gx", axis=0, tiled=True)
    normed = (scaled * gain_piece.astype(jnp.float32)[None, :]).astype(jnp.bfloat16)
    query_raw = jnp.dot(normed, query_piece, preferred_element_type=jnp.float32)
    key_raw = jnp.dot(normed, key_piece, preferred_element_type=jnp.float32)
    value_raw = jnp.dot(normed, value_piece, preferred_element_type=jnp.float32)
    queries = rotate(query_raw.reshape(count, -1, head_size), positions).astype(jnp.bfloat16)
    keys = rotate(key_raw[:, None, :], positions)[:, 0, :].astype(jnp.bfloat16)
    values = value_raw.astype(jnp.bfloat16)
    mixed = attend(queries, keys, values, segment_ids, positions)
    inner_cols = lax.all_gather(o_weight[0], "gz", axis=1, tiled=True)
    middle_cols = lax.all_gather(inner_cols, "gy", axis=1, tiled=True)
    branch = jnp.dot(
        mixed,
        lax.all_gather(middle_cols, "gx", axis=1, tiled=True),
        preferred_element_type=jnp.float32,
    )
    current = (widened + branch).astype(jnp.bfloat16)
    return current


def solution(mesh):
    in_specs = (
        P(("gx", "gy", "gz"), None),
        P(("gx", "gy", "gz")),
        P(("gx", "gy", "gz")),
        P(None, ("gx", "gy", "gz")),
        P(None, ("gx", "gy", "gz"), None),
        P(None, ("gx", "gy", "gz"), None),
        P(None, ("gx", "gy", "gz"), None),
        P(None, None, ("gx", "gy", "gz")),
    )
    out_specs = P(("gx", "gy", "gz"), None)
    return jax.shard_map(body, mesh=mesh, in_specs=in_specs, out_specs=out_specs, check_vma=False)
```

profile of v0, /device:TPU:0, one launch (start us, length us, event | category | flops | bytes accessed | tf_op | source)
XLA Modules:
  0.0 307.4 jit_solution(744721059821343803)
XLA Ops:
  6.5 12.0 %all-gather.9 = bf16[1,512,512]{2,1,0:T(8,128)(2,1)} all-gather(bf16[1,256,512]{2,1,0:T(8,128)(2,1)} %param.12), channel_id=11, replica_groups=mesh['gx'=4,'gy'=4,'gz'=2] {'gz'}, dimensions={1}, use_global_device_ids=true | all-gather | bytes 786432 | tf_op jit(solution)/shard_map/all_gather | solution.py:44
  18.6 0.0 all-gather.30.cloned.1.call-start
  18.7 8.5 %all-gather.12 = bf16[1,512,512]{2,1,0:T(8,128)(2,1)} all-gather(bf16[1,512,256]{2,1,0:T(8,128)(2,1)} %param.15), channel_id=14, replica_groups=mesh['gx'=4,'gy'=4,'gz'=2] {'gz'}, dimensions={2}, use_global_device_ids=true | all-gather | bytes 786432 | tf_op jit(solution)/shard_map/all_gather | solution.py:66
  27.2 0.0 all-gather.24.cloned.1.call-start
  27.2 5.2 %all-gather.6 = bf16[1,512,128]{2,1,0:T(8,128)(2,1)S(1)} all-gather(bf16[1,256,128]{2,1,0:T(8,128)(2,1)} %param.13), channel_id=8, replica_groups=mesh['gx'=4,'gy'=4,'gz'=2] {'gz'}, dimensions={1}, use_global_device_ids=true | all-gather | bytes 196608 | tf_op jit(solution)/shard_map/all_gather | solution.py:45
  32.4 23.9 %all-gather.7 = bf16[1,2048,128]{2,1,0:T(8,128)(2,1)} all-gather(bf16[1,512,128]{2,1,0:T(8,128)(2,1)S(1)} %all-gather.6), channel_id=9, replica_groups=mesh['gx'=4,'gy'=4,'gz'=2] {'gy'}, dimensions={1}, use_global_device_ids=true | all-gather | bytes 655360 | tf_op jit(solution)/shard_map/all_gather | solution.py:51
  56.2 0.0 all-gather.28.cloned.1.call-start
  56.3 16.9 %all-gather.26.cloned.1.call-done = bf16[1,2048,512]{2,1,0:T(8,128)(2,1)} async-done(((bf16[1,512,512]{2,1,0:T(8,128)(2,1)}), bf16[1,2048,512]{2,1,0:T(8,128)(2,1)}) %all-gather.26.cloned.1.call-update) | async-done | bytes 2097168 | tf_op jit(solution)/shard_map/all_gather | solution.py:50
  73.3 4.9 %all-gather.3 = bf16[1,512,128]{2,1,0:T(8,128)(2,1)S(1)} all-gather(bf16[1,256,128]{2,1,0:T(8,128)(2,1)S(1)} %copy-done), channel_id=5, replica_groups=mesh['gx'=4,'gy'=4,'gz'=2] {'gz'}, dimensions={1}, use_global_device_ids=true | all-gather | bytes 196608 | tf_op jit(solution)/shard_map/all_gather | solution.py:46
  78.2 20.2 %all-gather.4 = bf16[1,2048,128]{2,1,0:T(8,128)(2,1)} all-gather(bf16[1,512,128]{2,1,0:T(8,128)(2,1)S(1)} %all-gather.3), channel_id=6, replica_groups=mesh['gx'=4,'gy'=4,'gz'=2] {'gy'}, dimensions={1}, use_global_device_ids=true | all-gather | bytes 655360 | tf_op jit(solution)/shard_map/all_gather | solution.py:52
  98.4 0.0 all-gather.32.cloned.1.call-start
  98.4 26.2 %all-gather.30.cloned.1.call-done = bf16[1,512,2048]{2,1,0:T(8,128)(2,1)} async-done(((bf16[1,512,512]{2,1,0:T(8,128)(2,1)}), bf16[1,512,2048]{2,1,0:T(8,128)(2,1)}) %all-gather.30.cloned.1.call-update) | async-done | bytes 2097168 | tf_op jit(solution)/shard_map/all_gather | solution.py:67
  124.7 4.2 %all-gather = bf16[1,512]{1,0:T(2,128)(2,1)S(1)} all-gather(bf16[1,256]{1,0:T(2,128)(2,1)S(1)} %copy-done.3), channel_id=2, replica_groups=mesh['gx'=4,'gy'=4,'gz'=2] {'gz'}, dimensions={1}, use_global_device_ids=true | all-gather | bytes 1536 | tf_op jit(solution)/shard_map/all_gather | solution.py:43
  128.9 11.9 %all-gather.1 = bf16[1,2048]{1,0:T(2,128)(2,1)S(1)} all-gather(bf16[1,512]{1,0:T(2,128)(2,1)S(1)} %all-gather), channel_id=3, replica_groups=mesh['gx'=4,'gy'=4,'gz'=2] {'gy'}, dimensions={1}, use_global_device_ids=true | all-gather | bytes 5120 | tf_op jit(solution)/shard_map/all_gather | solution.py:49
  140.9 5.5 %all-gather.2 = bf16[1,8192]{1,0:T(2,128)(2,1)S(1)} all-gather(bf16[1,2048]{1,0:T(2,128)(2,1)S(1)} %all-gather.1), channel_id=4, replica_groups=mesh['gx'=4,'gy'=4,'gz'=2] {'gx'}, dimensions={1}, use_global_device_ids=true | all-gather | bytes 20480 | tf_op jit(solution)/shard_map/all_gather | solution.py:54
  146.4 3.1 %fusion.2 = f32[256]{0:T(256)S(1)} fusion(bf16[256,8192]{1,0:T(8,128)(2,1)} %param.8), kind=kLoop, calls=%fused_computation.5 | loop fusion | flops 6291200 | bytes 4195328 | tf_op jit(solution)/shard_map/reduce_sum | solution.py:40
  149.6 0.1 compare_and_fusion
  149.7 0.3 multiply_cosine_fusion
  150.1 4.6 %fusion.8 = f32[256,128]{0,1:T(8,128)S(1)} fusion(bf16[1,8192,128]{2,1,0:T(8,128)(2,1)} %all-gather.24.cloned.1.call-done, bf16[256,8192]{1,0:T(8,128)(2,1)} %param.8, f32[8192]{0:T(1024)S(1)} %bitcast.83, f32[256]{0:T(256)S(1)} %add_rsqrt_fusion), kind=kOutput, calls=%fused_computation.11 | convolution fusion | flops 545259520 | bytes 6456320 | tf_op jit(solution)/shard_map/dot_general | solution.py:60
  154.7 0.1 copy.10
  154.8 0.1 copy.9
  154.9 52.9 %all-gather.28.cloned.1.call-done = bf16[1,8192,512]{2,1,0:T(8,128)(2,1)} async-done(((bf16[1,2048,512]{2,1,0:T(8,128)(2,1)}), bf16[1,8192,512]{2,1,0:T(8,128)(2,1)}) %all-gather.28.cloned.1.call-update) | async-done | bytes 8388624 | tf_op jit(solution)/shard_map/all_gather | solution.py:55
  207.9 7.0 %fusion.6 = f32[256,512]{1,0:T(8,128)S(1)} fusion(bf16[1,8192,512]{2,1,0:T(8,128)(2,1)} %all-gather.28.cloned.1.call-done, bf16[256,8192]{1,0:T(8,128)(2,1)} %param.8, f32[8192]{0:T(1024)S(1)} %bitcast.84, f32[256]{0:T(256)S(1)} %add_rsqrt_fusion), kind=kOutput, calls=%fused_computation.9 | convolution fusion | flops 2155872256 | bytes 13140992 | tf_op jit(solution)/shard_map/dot_general | solution.py:59
  214.9 0.2 reshape.93
  215.1 0.3 slice_negate_fusion
  215.4 0.4 maximum_multiply_fusion
  215.8 0.1 mul.85
  215.9 0.5 fusion.44
  216.4 15.4 %all-gather.22.cloned.1.call-done = bf16[1,8192,128]{2,1,0:T(8,128)(2,1)} async-done(((bf16[1,2048,128]{2,1,0:T(8,128)(2,1)}), bf16[1,8192,128]{2,1,0:T(8,128)(2,1)}) %all-gather.22.cloned.1.call-update) | async-done | bytes 2097168 | tf_op jit(solution)/shard_map/all_gather | solution.py:57
  231.9 4.7 %convolution_convert_fusion = bf16[128,4,256]{2,0,1:T(8,128)(2,1)S(1)} fusion(bf16[1,8192,128]{2,1,0:T(8,128)(2,1)} %all-gather.22.cloned.1.call-done, f32[4,256,256]{1,2,0:T(8,128)S(1)} %get-tuple-element.15, f32[4,256]{1,0:T(4,128)S(1)} %get-tuple-element.14, bf16[256,8192]{1,0:T(8,128)(2,1)} %param.8, f32[8192]{0:T(1024)S(1)} %bitcast.85, ...), kind=kOutput, calls=%fused_computation.20 | convolution fusion | flops 613056512 | bytes 7640064 | tf_op jit(solution)/shard_map/hts,sd->thd/dot_general | solution.py:31
  236.5 55.0 %all-gather.32.cloned.1.call-done = bf16[1,512,8192]{2,1,0:T(8,128)(2,1)} async-done(((bf16[1,512,2048]{2,1,0:T(8,128)(2,1)}), bf16[1,512,8192]{2,1,0:T(8,128)(2,1)}) %all-gather.32.cloned.1.call-update) | async-done | bytes 8388624 | tf_op jit(solution)/shard_map/all_gather | solution.py:70
  291.6 9.0 %fusion.1 = bf16[256,8192]{1,0:T(8,128)(2,1)} fusion(bf16[256,512]{0,1:T(8,128)(2,1)S(1)} %bitcast.82, bf16[256,8192]{1,0:T(8,128)(2,1)} %param.8, bf16[1,512,8192]{2,1,0:T(8,128)(2,1)} %all-gather.32.cloned.1.call-done), kind=kOutput, calls=%fused_computation.4 | convolution fusion | flops 2153775104 | bytes 17039360 | tf_op jit(solution)/shard_map/dot_general | solution.py:68
  (23 shorter events, 0.3 us)
Async XLA Ops:
  6.5 66.7 %copy-start = (bf16[1,256,128]{2,1,0:T(8,128)(2,1)S(1)}, bf16[1,256,128]{2,1,0:T(8,128)(2,1)}, u32[]{:S(2)}) copy-start(bf16[1,256,128]{2,1,0:T(8,128)(2,1)} %param.14) | copy-start | bytes 196612
  6.5 66.6 %all-gather.26.cloned.1.call-start = ((), (), s32[]{:S(2)}) async-start(), calls=%async_computation.2 | async-start | bytes 2621440 | tf_op jit(solution)/shard_map/all_gather | solution.py:50
  18.6 106.1 %copy-start.3 = (bf16[1,256]{1,0:T(2,128)(2,1)S(1)}, bf16[1,256]{1,0:T(2,128)(2,1)}, u32[]{:S(2)}) copy-start(bf16[1,256]{1,0:T(2,128)(2,1)} %param.11) | copy-start | bytes 1540
  18.6 127.8 %copy-start.1 = (s32[256]{0:T(256)S(1)}, s32[256]{0:T(256)}, u32[]{:S(2)}) copy-start(s32[256]{0:T(256)} %param.10) | copy-start | bytes 3076
  18.6 106.0 %all-gather.30.cloned.1.call-start = ((), (), s32[]{:S(2)}) async-start(), calls=%async_computation.4 | async-start | bytes 2621440 | tf_op jit(solution)/shard_map/all_gather | solution.py:67
  27.2 122.9 %all-gather.24.cloned.1.call-start = ((), (), s32[]{:S(2)}) async-start(), calls=%async_computation.1 | async-start | bytes 2621440 | tf_op jit(solution)/shard_map/all_gather | solution.py:56
  56.2 151.6 %all-gather.28.cloned.1.call-start = ((), (), s32[]{:S(2)}) async-start(), calls=%async_computation.3 | async-start | bytes 10485760 | tf_op jit(solution)/shard_map/all_gather | solution.py:55
  73.2 76.4 %copy-start.2 = (s32[256]{0:T(256)S(1)}, s32[256]{0:T(256)}, u32[]{:S(2)}) copy-start(s32[256]{0:T(256)} %param.9) | copy-start | bytes 3076
  73.2 158.7 %all-gather.22.cloned.1.call-start = ((), (), s32[]{:S(2)}) async-start(), calls=%async_computation | async-start | bytes 2621440 | tf_op jit(solution)/shard_map/all_gather | solution.py:57
  98.4 193.2 %all-gather.32.cloned.1.call-start = ((), (), s32[]{:S(2)}) async-start(), calls=%async_computation.5 | async-start | bytes 10485760 | tf_op jit(solution)/shard_map/all_gather | solution.py:70
Sparse Core Ops, SparseCore 0:
  18.7 54.3 all-gather.25
  74.7 49.8 all-gather.29
  126.2 21.8 all-gather.23
  149.6 58.2 all-gather.27
  209.3 22.5 all-gather.21
  233.3 58.2 all-gather.31
where the time goes:
time: 308 us; the launch traced here: 307 us
  waiting for transfers between devices  167 us (54%)
  blocking collectives  96.3 us (31%)
  matrix products  25.9 us (8%)
  between operations  13.6 us (4%)
  other arithmetic  4.37 us (1%)
    all_gather x1, waiting for transfers between devices, body(): lax.all_gather(middle_cols, 'gx', axis=1, tiled=True)  55 us
    all_gather x1, waiting for transfers between devices, body(): query_piece = lax.all_gather(middle[1], 'gx', axis=0, tiled=True)  52.9 us
    all_gather x1, waiting for transfers between devices, body(): middle_cols = lax.all_gather(inner_cols, 'gy', axis=1, tiled=True)  26.2 us
    all_gather x1, blocking collectives, body(): lax.all_gather(inner[2], 'gy', axis=0, tiled=True)  23.9 us
    all_gather x1, blocking collectives, body(): lax.all_gather(inner[3], 'gy', axis=0, tiled=True)  20.2 us
    all_gather x1, waiting for transfers between devices, body(): lax.all_gather(inner[1], 'gy', axis=0, tiled=True)  16.9 us
    all_gather x1, waiting for transfers between devices, body(): value_piece = lax.all_gather(middle[3], 'gx', axis=0, tiled=True)  15.4 us
    all_gather x1, blocking collectives, body(): lax.all_gather(q_weight[0], 'gz', axis=0, tiled=True)  12 us
  transfers between devices with their start and end apart: 6, of which 5 were waited for; matrix products, arithmetic and copies ran while one was open for 7% of the time, Pallas kernels for 0%

commit v1 on v0

--- a/solution.py
+++ b/solution.py
@@ -1,8 +1,27 @@
+import functools
 import math
 import jax
 import jax.numpy as jnp
 from jax import lax
 from jax.sharding import PartitionSpec as P
+
+
+def bring_the_case(x0, at_axis):
+    num = jax.lax.axis_size("gx")
+    crops = [(q, (q + 1) % num) for q in range(num)]
+
+    def list_ways(now):
+        if len(now) == num:
+            return now
+        return list_ways([jax.lax.ppermute(now[0], axis_name="gx", perm=crops), *now])
+
+    kept_arr = jnp.concatenate(list_ways([x0]), axis=at_axis)
+    return jnp.roll(
+        kept_arr, shift=(jax.lax.axis_index("gx") + 1) * x0.shape[at_axis], axis=at_axis
+    )
+
+
+number_sizes = functools.partial(bring_the_case, at_axis=0)
 
 
 def rotate(values, positions):
@@ -52,7 +71,7 @@
         lax.all_gather(inner[3], "gy", axis=0, tiled=True),
     )
     gain_piece = lax.all_gather(middle[0], "gx", axis=0, tiled=True)
-    query_piece = lax.all_gather(middle[1], "gx", axis=0, tiled=True)
+    query_piece = number_sizes(middle[1])
     key_piece = lax.all_gather(middle[2], "gx", axis=0, tiled=True)
     value_piece = lax.all_gather(middle[3], "gx", axis=0, tiled=True)
     normed = (scaled * gain_piece.astype(jnp.float32)[None, :]).astype(jnp.bfloat16)

time: 308 us -> 301 us (0.977)
  waiting for transfers between devices: 167 us -> 134 us
  blocking collectives: 96.3 us -> 118 us
  local copies, waits for them, and re-layouts: 0.48 us -> 8.09 us
  matrix products: 25.9 us -> 21.2 us
    ppermute x0 -> x3, waiting for transfers between devices: none -> 89.7 us  [list_ways(): jax.lax.ppermute(now[0], axis_name='gx', perm=crops)]
    all_gather x1, waiting for transfers between devices: 55 us -> 0.02 us  [body(): lax.all_gather(middle_cols, 'gx', axis=1, tiled=True)]
    all_gather x1 -> x0, waiting for transfers between devices: 52.9 us -> none  [body(): query_piece = lax.all_gather(middle[1], 'gx', axis=0, tiled=True)]
    all_gather x1, waiting for transfers between devices: 16.9 us -> 43.6 us  [body(): lax.all_gather(inner[1], 'gy', axis=0, tiled=True)]
    all_gather x1, waiting for transfers between devices: 26.2 us -> 0.02 us  [body(): middle_cols = lax.all_gather(inner_cols, 'gy', axis=1, tiled=True)]
    all_gather x1, blocking collectives: 5.47 us -> 25.7 us  [body(): gain_piece = lax.all_gather(middle[0], 'gx', axis=0, tiled=True)]
    all_gather x1, waiting for transfers between devices: 15.4 us -> 0.02 us  [body(): value_piece = lax.all_gather(middle[3], 'gx', axis=0, tiled=True)]
    unnamed x8 -> x19, local copies, waits for them, and re-layouts: 0.02 us -> 7.5 us
  transfers between devices with their start and end apart: 6 -> 8, of which waited for: 5 -> 3; matrix products, arithmetic and copies ran while one was open for 7% -> 8% of each run, Pallas kernels for 0% -> 0%
where the time goes in v1:
time: 301 us; the launch traced here: 300 us
  waiting for transfers between devices  134 us (45%)
  blocking collectives  118 us (39%)
  matrix products  21.2 us (7%)
  between operations  13.4 us (4%)
  local copies, waits for them, and re-layouts  8.09 us (3%)
  other arithmetic  5.1 us (2%)
    ppermute x3, waiting for transfers between devices, list_ways(): jax.lax.ppermute(now[0], axis_name='gx', perm=crops)  89.7 us
    all_gather x1, waiting for transfers between devices, body(): lax.all_gather(inner[1], 'gy', axis=0, tiled=True)  43.6 us
    all_gather x1, blocking collectives, body(): gain_piece = lax.all_gather(middle[0], 'gx', axis=0, tiled=True)  25.7 us
    all_gather x1, blocking collectives, body(): lax.all_gather(inner[2], 'gy', axis=0, tiled=True)  23.9 us
    all_gather x1, blocking collectives, body(): lax.all_gather(inner[3], 'gy', axis=0, tiled=True)  21.3 us
    all_gather x1, blocking collectives, body(): inner_cols = lax.all_gather(o_weight[0], 'gz', axis=1, tiled=True)  12 us
    all_gather x1, blocking collectives, body(): lax.all_gather(inner[0], 'gy', axis=0, tiled=True)  11.9 us
    dot_general x1, matrix products, body(): jnp.dot(mixed, lax.all_gather(middle_cols, 'gx', axis=1, tiled=True), pre...  9.02 us
  transfers between devices with their start and end apart: 8, of which 3 were waited for; matrix products, arithmetic and copies ran while one was open for 8% of the time, Pallas kernels for 0%

profile of v1, /device:TPU:0, one launch (start us, length us, event | category | flops | bytes accessed | tf_op | source)
XLA Modules:
  0.0 300.1 jit_solution(5459810443050345550)
XLA Ops:
  6.5 12.0 %all-gather.11 = bf16[1,512,512]{2,1,0:T(8,128)(2,1)} all-gather(bf16[1,512,256]{2,1,0:T(8,128)(2,1)} %param.15), channel_id=13, replica_groups=mesh['gx'=4,'gy'=4,'gz'=2] {'gz'}, dimensions={2}, use_global_device_ids=true | all-gather | bytes 786432 | tf_op jit(solution)/shard_map/all_gather | solution.py:85
  18.6 8.5 %all-gather.9 = bf16[1,512,512]{2,1,0:T(8,128)(2,1)} all-gather(bf16[1,256,512]{2,1,0:T(8,128)(2,1)} %param.12), channel_id=11, replica_groups=mesh['gx'=4,'gy'=4,'gz'=2] {'gz'}, dimensions={1}, use_global_device_ids=true | all-gather | bytes 786432 | tf_op jit(solution)/shard_map/all_gather | solution.py:63
  27.2 5.1 %all-gather.6 = bf16[1,512,128]{2,1,0:T(8,128)(2,1)S(1)} all-gather(bf16[1,256,128]{2,1,0:T(8,128)(2,1)} %param.13), channel_id=8, replica_groups=mesh['gx'=4,'gy'=4,'gz'=2] {'gz'}, dimensions={1}, use_global_device_ids=true | all-gather | bytes 196608 | tf_op jit(solution)/shard_map/all_gather | solution.py:64
  32.3 23.9 %all-gather.7 = bf16[1,2048,128]{2,1,0:T(8,128)(2,1)} all-gather(bf16[1,512,128]{2,1,0:T(8,128)(2,1)S(1)} %all-gather.6), channel_id=9, replica_groups=mesh['gx'=4,'gy'=4,'gz'=2] {'gy'}, dimensions={1}, use_global_device_ids=true | all-gather | bytes 655360 | tf_op jit(solution)/shard_map/all_gather | solution.py:70
  56.3 5.1 %all-gather.3 = bf16[1,512,128]{2,1,0:T(8,128)(2,1)S(1)} all-gather(bf16[1,256,128]{2,1,0:T(8,128)(2,1)} %param.14), channel_id=5, replica_groups=mesh['gx'=4,'gy'=4,'gz'=2] {'gz'}, dimensions={1}, use_global_device_ids=true | all-gather | bytes 196608 | tf_op jit(solution)/shard_map/all_gather | solution.py:65
  61.4 21.3 %all-gather.4 = bf16[1,2048,128]{2,1,0:T(8,128)(2,1)} all-gather(bf16[1,512,128]{2,1,0:T(8,128)(2,1)S(1)} %all-gather.3), channel_id=6, replica_groups=mesh['gx'=4,'gy'=4,'gz'=2] {'gy'}, dimensions={1}, use_global_device_ids=true | all-gather | bytes 655360 | tf_op jit(solution)/shard_map/all_gather | solution.py:71
  82.9 0.5 all-gather.28.cloned.1.call-update
  83.4 43.6 %all-gather.24.cloned.1.call-done = bf16[1,2048,512]{2,1,0:T(8,128)(2,1)} async-done(((bf16[1,512,512]{2,1,0:T(8,128)(2,1)}), bf16[1,2048,512]{2,1,0:T(8,128)(2,1)}) %all-gather.24.cloned.1.call-update) | async-done | bytes 2097168 | tf_op jit(solution)/shard_map/all_gather | solution.py:69
  126.9 36.9 %collective-permute-done = bf16[2048,512]{1,0:T(8,128)(2,1)S(1)} collective-permute-done((bf16[2048,512]{1,0:T(8,128)(2,1)}, bf16[2048,512]{1,0:T(8,128)(2,1)S(1)}, u32[]{:S(2)}, u32[]{:S(2)}) %collective-permute-start) | collective-permute-done | bytes 2097184 | tf_op jit(solution)/shard_map/ppermute | solution.py:16
  163.9 4.4 %all-gather = bf16[1,512]{1,0:T(2,128)(2,1)S(1)} all-gather(bf16[1,256]{1,0:T(2,128)(2,1)} %param.11), channel_id=2, replica_groups=mesh['gx'=4,'gy'=4,'gz'=2] {'gz'}, dimensions={1}, use_global_device_ids=true | all-gather | bytes 1536 | tf_op jit(solution)/shard_map/all_gather | solution.py:62
  168.3 11.9 %all-gather.1 = bf16[1,2048]{1,0:T(2,128)(2,1)S(1)} all-gather(bf16[1,512]{1,0:T(2,128)(2,1)S(1)} %all-gather), channel_id=3, replica_groups=mesh['gx'=4,'gy'=4,'gz'=2] {'gy'}, dimensions={1}, use_global_device_ids=true | all-gather | bytes 5120 | tf_op jit(solution)/shard_map/all_gather | solution.py:68
  180.2 25.7 %all-gather.2 = bf16[1,8192]{1,0:T(2,128)(2,1)S(1)} all-gather(bf16[1,2048]{1,0:T(2,128)(2,1)S(1)} %all-gather.1), channel_id=4, replica_groups=mesh['gx'=4,'gy'=4,'gz'=2] {'gx'}, dimensions={1}, use_global_device_ids=true | all-gather | bytes 20480 | tf_op jit(solution)/shard_map/all_gather | solution.py:73
  206.0 0.7 convert_element_type.43
  206.7 0.2 collective-permute-start.2
  206.9 3.2 %fusion.2 = f32[256]{0:T(256)S(1)} fusion(bf16[256,8192]{1,0:T(8,128)(2,1)} %param.8), kind=kLoop, calls=%fused_computation.5 | loop fusion | flops 6291200 | bytes 4195328 | tf_op jit(solution)/shard_map/reduce_sum | solution.py:59
  210.2 0.3 multiply_cosine_fusion
  210.6 4.6 %fusion.8 = f32[256,128]{0,1:T(8,128)S(1)} fusion(bf16[1,8192,128]{2,1,0:T(8,128)(2,1)} %all-gather.22.cloned.1.call-done, bf16[256,8192]{1,0:T(8,128)(2,1)} %param.8, f32[8192]{0:T(1024)S(1)} %bitcast.84, f32[256]{0:T(256)S(1)} %add_rsqrt_fusion), kind=kOutput, calls=%fused_computation.11 | convolution fusion | flops 545259520 | bytes 6456320 | tf_op jit(solution)/shard_map/dot_general | solution.py:79
  215.5 52.8 %collective-permute-done.2 = bf16[2048,512]{1,0:T(8,128)(2,1)} collective-permute-done((bf16[2048,512]{1,0:T(8,128)(2,1)}, bf16[2048,512]{1,0:T(8,128)(2,1)}, u32[]{:S(2)}, u32[]{:S(2)}) %collective-permute-start.2) | collective-permute-done | bytes 2097184 | tf_op jit(solution)/shard_map/ppermute | solution.py:16
  268.2 1.7 constant_dynamic-update-slice_fusion.7
  270.0 1.7 constant_dynamic-update-slice_fusion.6
  271.7 0.1 constant_dynamic-update-slice_fusion.5
  271.9 0.1 constant_dynamic-update-slice_fusion.4
  272.0 1.9 constant_dynamic-update-slice_fusion.3
  273.9 1.7 constant_dynamic-update-slice_fusion.2
  275.6 0.1 constant_dynamic-update-slice_fusion.1
  275.9 2.4 fusion.6
  278.3 0.2 reshape.93
  278.5 0.3 slice_negate_fusion
  278.8 0.4 maximum_multiply_fusion
  279.3 0.5 fusion.45
  279.9 4.7 %convolution_convert_fusion = bf16[128,4,256]{2,0,1:T(8,128)(2,1)S(1)} fusion(bf16[1,8192,128]{2,1,0:T(8,128)(2,1)} %all-gather.20.cloned.1.call-done, f32[4,256,256]{1,2,0:T(8,128)S(1)} %get-tuple-element.15, f32[4,256]{1,0:T(4,128)S(1)} %get-tuple-element.14, bf16[256,8192]{1,0:T(8,128)(2,1)} %param.8, f32[8192]{0:T(1024)S(1)} %bitcast.86, ...), kind=kOutput, calls=%fused_computation.20 | convolution fusion | flops 613056512 | bytes 7640064 | tf_op jit(solution)/shard_map/hts,sd->thd/dot_general | solution.py:50
  284.6 9.0 %fusion.1 = bf16[256,8192]{1,0:T(8,128)(2,1)} fusion(bf16[256,512]{0,1:T(8,128)(2,1)S(1)} %bitcast.83, bf16[256,8192]{1,0:T(8,128)(2,1)} %param.8, bf16[1,512,8192]{2,1,0:T(8,128)(2,1)} %all-gather.28.cloned.1.call-done), kind=kOutput, calls=%fused_computation.4 | convolution fusion | flops 2153775104 | bytes 17039360 | tf_op jit(solution)/shard_map/dot_general | solution.py:87
  (38 shorter events, 1.0 us)
Async XLA Ops:
  6.5 203.5 %copy-start.4 = (s32[256]{0:T(256)S(1)}, s32[256]{0:T(256)}, u32[]{:S(2)}) copy-start(s32[256]{0:T(256)} %param.10) | copy-start | bytes 3076
  6.5 203.5 %copy-start.5 = (s32[256]{0:T(256)S(1)}, s32[256]{0:T(256)}, u32[]{:S(2)}) copy-start(s32[256]{0:T(256)} %param.9) | copy-start | bytes 3076
  6.5 76.3 %all-gather.26.cloned.1.call-start = ((), (), s32[]{:S(2)}) async-start(), calls=%async_computation.3 | async-start | bytes 2621440 | tf_op jit(solution)/shard_map/all_gather | solution.py:86
  18.6 108.4 %all-gather.24.cloned.1.call-start = ((), (), s32[]{:S(2)}) async-start(), calls=%async_computation.2 | async-start | bytes 2621440 | tf_op jit(solution)/shard_map/all_gather | solution.py:69
  27.1 183.4 %all-gather.22.cloned.1.call-start = ((), (), s32[]{:S(2)}) async-start(), calls=%async_computation.1 | async-start | bytes 2621440 | tf_op jit(solution)/shard_map/all_gather | solution.py:75
  56.2 223.6 %all-gather.20.cloned.1.call-start = ((), (), s32[]{:S(2)}) async-start(), calls=%async_computation | async-start | bytes 2621440 | tf_op jit(solution)/shard_map/all_gather | solution.py:76
  82.8 201.8 %all-gather.28.cloned.1.call-start = ((), (), s32[]{:S(2)}) async-start(), calls=%async_computation.4 | async-start | bytes 10485760 | tf_op jit(solution)/shard_map/all_gather | solution.py:89
  126.9 36.9 %collective-permute-start = (bf16[2048,512]{1,0:T(8,128)(2,1)}, bf16[2048,512]{1,0:T(8,128)(2,1)S(1)}, u32[]{:S(2)}, u32[]{:S(2)}) collective-permute-start(bf16[2048,512]{1,0:T(8,128)(2,1)} %bitcast.79), channel_id=1, source_target_pairs={{0,8},{8,16},{16,24},{24,0},{1,9},{9,17},{17,25},{25,1},{2,10},{10... | collective-permute-start | bytes 6291464 | tf_op jit(solution)/shard_map/ppermute | solution.py:16
  163.8 46.7 %copy-start.2 = (bf16[2048,512]{1,0:T(8,128)(2,1)}, bf16[2048,512]{1,0:T(8,128)(2,1)S(1)}, u32[]{:S(2)}) copy-start(bf16[2048,512]{1,0:T(8,128)(2,1)S(1)} %collective-permute-done) | copy-start | bytes 6291460
  163.8 42.8 %collective-permute-start.1 = (bf16[2048,512]{1,0:T(8,128)(2,1)S(1)}, bf16[2048,512]{1,0:T(8,128)(2,1)}, u32[]{:S(2)}, u32[]{:S(2)}) collective-permute-start(bf16[2048,512]{1,0:T(8,128)(2,1)S(1)} %collective-permute-done), channel_id=1, source_target_pairs={{0,8},{8,16},{16,24},{24,0},{1,9},{9,17},{17,25},{25,1},{2,10},{10... | collective-permute-start | bytes 6291464 | tf_op jit(solution)/shard_map/ppermute | solution.py:16
  206.7 61.5 %collective-permute-start.2 = (bf16[2048,512]{1,0:T(8,128)(2,1)}, bf16[2048,512]{1,0:T(8,128)(2,1)}, u32[]{:S(2)}, u32[]{:S(2)}) collective-permute-start(bf16[2048,512]{1,0:T(8,128)(2,1)} %collective-permute-done.1), channel_id=1, source_target_pairs={{0,8},{8,16},{16,24},{24,0},{1,9},{9,17},{17,25},{25,1},{2,10},{10... | collective-permute-start | bytes 6291464 | tf_op jit(solution)/shard_map/ppermute | solution.py:16
  215.2 56.6 %copy-start.1 = (bf16[1,2048,512]{2,1,0:T(8,128)(2,1)S(1)}, bf16[1,2048,512]{2,1,0:T(8,128)(2,1)}, u32[]{:S(2)}) copy-start(bf16[1,2048,512]{2,1,0:T(8,128)(2,1)} %all-gather.24.cloned.1.call-done) | copy-start | bytes 6291460
  215.5 56.2 %copy-start.3 = (bf16[2048,512]{1,0:T(8,128)(2,1)S(1)}, bf16[2048,512]{1,0:T(8,128)(2,1)}, u32[]{:S(2)}) copy-start(bf16[2048,512]{1,0:T(8,128)(2,1)} %copy-done.2) | copy-start | bytes 6291460
  272.0 3.9 %copy-start = (bf16[256,8192]{1,0:T(8,128)(2,1)S(1)}, bf16[256,8192]{1,0:T(8,128)(2,1)}, u32[]{:S(2)}) copy-start(bf16[256,8192]{1,0:T(8,128)(2,1)} %param.8) | copy-start | bytes 12582916
Sparse Core Ops, SparseCore 0:
  18.7 62.2 all-gather.25
  82.6 44.2 all-gather.23
  128.5 27.0 all-gather.21
  157.1 28.2 all-gather.19
  186.8 78.4 all-gather.27
